TPU v7x, 16 devices: a 4x2x1 block of a 4x4x8 slice. The times are simulated.
16 devices in a mesh: data: 2 (over y, z), time: 8 (over x, core).
Axes of the slice: x: 4, y: 2, z: 1, core: 2. Of those that a mesh axis runs over, the one named last changes fastest.
The devices are a block of a 4x4x8 slice.
Arguments:
- x_init: float32 [8, 256, 16], P('data'), parts along dimension 0
- w_in: bfloat16 [16, 768], replicated
- w_out: bfloat16 [768, 16], replicated
- mod_scale: bfloat16 [24, 768], P('time')
- mod_shift: bfloat16 [24, 768], P('time')
- step_size: float32 [24], P('time')
Outputs:
- output: float32 [24, 8, 256, 16], P('time', 'data'), parts along dimension 1
There are 2 independent parts. A program takes and returns all parts, laid end to end along the dimension named above; an argument that names none is the same for every part.
All inputs are finite; a program needn't handle non-finite values.
Results may differ from a plain program's by a relative error of at most 0.001.
Values are sent between devices in bfloat16 or wider.
A program may use at most 768 MiB of HBM per device.

v0:
```python
import jax
import jax.numpy as jnp
from jax import lax
from jax.sharding import PartitionSpec as P

SWEEPS = 4


def solution(mesh):
    n_time = mesh.shape['time']

    def per_device(x_init, w_in, w_out, mod_scale, mod_shift, step_size):
        lat_shape = x_init.shape
        flat_len = x_init.size
        gain_rows = (1.0 + mod_scale.astype(jnp.float32))[:, None, None, :]
        shift_rows = mod_shift.astype(jnp.float32)[:, None, None, :]
        step_rows = step_size[:, None, None, None]
        latent = jnp.broadcast_to(x_init[None], (mod_scale.shape[0],) + lat_shape)
        for sweep_idx in range(SWEEPS):
            pre_act = jnp.einsum('kbnc,cd->kbnd', latent.astype(jnp.bfloat16), w_in, preferred_element_type=jnp.float32)
            hidden = jax.nn.gelu(pre_act * gain_rows + shift_rows, approximate=True).astype(jnp.bfloat16)
            drifts = step_rows * jnp.einsum('kbnd,dc->kbnc', hidden, w_out, preferred_element_type=jnp.float32)
            local_cum = jnp.cumsum(drifts, axis=0)
            dev_total = local_cum[-1].reshape(n_time, flat_len // n_time)
            columns = lax.all_to_all(dev_total, 'time', 0, 0, tiled=True)
            col_prefix = jnp.cumsum(columns, axis=0) - columns
            offsets = lax.all_to_all(col_prefix, 'time', 0, 0, tiled=True).reshape(lat_shape)
            latent = x_init[None] + offsets[None] + (local_cum - drifts)
        return latent

    return jax.shard_map(per_device, mesh=mesh, in_specs=(P('data'), P(), P(), P('time'), P('time'), P('time')), out_specs=P('time', 'data'), check_vma=False)
```

profile of v0, /device:TPU:112, one launch (start us, length us, event | category | flops | bytes accessed | tf_op | source)
XLA Modules:
  0.0 96.0 jit_solution(4331722932200928559)
XLA Ops:
  0.0 0.7 convert_add_fusion
  0.7 0.7 convert_element_type.33
  1.4 0.8 convert_element_type.31
  2.2 4.8 %fusion.48 = f32[3,4,256,16]{2,3,1,0:T(8,128)S(1)} fusion(f32[3,768]{1,0:T(4,128)S(1)} %convert_element_type.33, f32[3,768]{1,0:T(4,128)S(1)} %convert_add_fusion, f32[3]{0:T(128)} %param.11, bf16[4,256,16]{1,2,0:T(8,128)(2,1)S(1)} %convert_element_type.31, bf16[768,16]{0,1:T(8,128)(2,1)S(1)} %copy-done, bf16[16,768]{1,0:T(8,128)(2,1)} %param.7), kind=kOutput, calls=%fused_computation.48 | convolution fusion | flops 176996352 | bytes 296972 | tf_op jit(solution)/shard_map/kbnd,dc->kbnc/dot_general | solution.py:22
  7.1 0.7 fusion.96
  7.8 0.2 copy.35
  8.0 0.2 all_to_all.52
  8.3 10.7 %all_to_all.64 = f32[8,1,2048]{2,1,0:T(1,128)S(1)} all-to-all(f32[8,1,2048]{2,1,0:T(1,128)S(1)} %all_to_all.52), channel_id=1, replica_groups=mesh['data'=2,'time'=8] {'time'}, dimensions={0} | all-to-all | bytes 131072 | tf_op jit(solution)/shard_map/all_to_all | solution.py:25
  19.0 8.1 %all_to_all.65 = f32[8,1,2048]{2,1,0:T(1,128)S(1)} all-to-all(f32[8,1,2048]{2,1,0:T(1,128)S(1)} %reduce-window_subtract_fusion.3), channel_id=1, replica_groups=mesh['data'=2,'time'=8] {'time'}, dimensions={0} | all-to-all | bytes 131072 | tf_op jit(solution)/shard_map/all_to_all | solution.py:27
  27.3 0.2 broadcast_in_dim_reshape.12
  27.7 0.4 copy-done.1
  28.2 4.4 %fusion.51 = f32[3,4,256,16]{2,3,1,0:T(8,128)S(1)} fusion(f32[3,768]{1,0:T(4,128)S(1)} %convert_element_type.33, f32[3,768]{1,0:T(4,128)S(1)} %convert_add_fusion, f32[3,4,256,16]{2,3,1,0:T(8,128)S(1)} %fusion.96, f32[3,4,256,16]{2,3,1,0:T(8,128)S(1)} %fusion.48, f32[4,256,16]{1,2,0:T(8,128)S(1)} %add.110, f32[3]{0:T(128)S(1)} %copy-done.3, ...), kind=kOutput, calls=%fused_computation.49 | convolution fusion | flops 177143808 | bytes 722956 | tf_op jit(solution)/shard_map/kbnd,dc->kbnc/dot_general | solution.py:22
  32.7 0.7 fusion.97
  33.4 0.2 copy.38
  33.6 0.2 all_to_all.53
  33.8 8.1 %all_to_all.66 = f32[8,1,2048]{2,1,0:T(1,128)S(1)} all-to-all(f32[8,1,2048]{2,1,0:T(1,128)S(1)} %all_to_all.53), channel_id=1, replica_groups=mesh['data'=2,'time'=8] {'time'}, dimensions={0} | all-to-all | bytes 131072 | tf_op jit(solution)/shard_map/all_to_all | solution.py:25
  41.9 8.1 %all_to_all.67 = f32[8,1,2048]{2,1,0:T(1,128)S(1)} all-to-all(f32[8,1,2048]{2,1,0:T(1,128)S(1)} %reduce-window_subtract_fusion.2), channel_id=1, replica_groups=mesh['data'=2,'time'=8] {'time'}, dimensions={0} | all-to-all | bytes 131072 | tf_op jit(solution)/shard_map/all_to_all | solution.py:27
  50.2 0.2 broadcast_in_dim_reshape.13
  50.6 4.5 %fusion.54 = f32[3,4,256,16]{2,3,1,0:T(8,128)S(1)} fusion(f32[3,768]{1,0:T(4,128)S(1)} %convert_element_type.33, f32[3,768]{1,0:T(4,128)S(1)} %convert_add_fusion, f32[3,4,256,16]{2,3,1,0:T(8,128)S(1)} %fusion.97, f32[3,4,256,16]{2,3,1,0:T(8,128)S(1)} %fusion.51, f32[4,256,16]{1,2,0:T(8,128)S(1)} %add.116, f32[3]{0:T(128)S(1)} %copy-done.3, ...), kind=kOutput, calls=%fused_computation.50 | convolution fusion | flops 177143808 | bytes 722956 | tf_op jit(solution)/shard_map/kbnd,dc->kbnc/dot_general | solution.py:22
  55.0 0.7 fusion.98
  55.9 0.2 all_to_all.54
  56.2 8.1 %all_to_all.68 = f32[8,1,2048]{2,1,0:T(1,128)S(1)} all-to-all(f32[8,1,2048]{2,1,0:T(1,128)S(1)} %all_to_all.54), channel_id=1, replica_groups=mesh['data'=2,'time'=8] {'time'}, dimensions={0} | all-to-all | bytes 131072 | tf_op jit(solution)/shard_map/all_to_all | solution.py:25
  64.3 8.1 %all_to_all.69 = f32[8,1,2048]{2,1,0:T(1,128)S(1)} all-to-all(f32[8,1,2048]{2,1,0:T(1,128)S(1)} %reduce-window_subtract_fusion.1), channel_id=1, replica_groups=mesh['data'=2,'time'=8] {'time'}, dimensions={0} | all-to-all | bytes 131072 | tf_op jit(solution)/shard_map/all_to_all | solution.py:27
  72.5 0.2 broadcast_in_dim_reshape.14
  72.9 4.4 %fusion.57 = f32[3,4,256,16]{2,3,1,0:T(8,128)S(1)} fusion(f32[3,768]{1,0:T(4,128)S(1)} %convert_element_type.33, f32[3,768]{1,0:T(4,128)S(1)} %convert_add_fusion, f32[3,4,256,16]{2,3,1,0:T(8,128)S(1)} %fusion.98, f32[3,4,256,16]{2,3,1,0:T(8,128)S(1)} %fusion.54, f32[4,256,16]{1,2,0:T(8,128)S(1)} %add.122, f32[3]{0:T(128)S(1)} %copy-done.3, ...), kind=kOutput, calls=%fused_computation.51 | convolution fusion | flops 177143808 | bytes 722956 | tf_op jit(solution)/shard_map/kbnd,dc->kbnc/dot_general | solution.py:22
  77.4 0.7 fusion.99
  78.1 0.2 copy.44
  78.3 0.2 all_to_all.55
  78.5 8.1 %all_to_all.70 = f32[8,1,2048]{2,1,0:T(1,128)S(1)} all-to-all(f32[8,1,2048]{2,1,0:T(1,128)S(1)} %all_to_all.55), channel_id=1, replica_groups=mesh['data'=2,'time'=8] {'time'}, dimensions={0} | all-to-all | bytes 131072 | tf_op jit(solution)/shard_map/all_to_all | solution.py:25
  86.6 8.1 %all_to_all.71 = f32[8,1,2048]{2,1,0:T(1,128)S(1)} all-to-all(f32[8,1,2048]{2,1,0:T(1,128)S(1)} %reduce-window_subtract_fusion), channel_id=1, replica_groups=mesh['data'=2,'time'=8] {'time'}, dimensions={0} | all-to-all | bytes 131072 | tf_op jit(solution)/shard_map/all_to_all | solution.py:27
  94.9 0.2 broadcast_in_dim_reshape.15
  95.3 0.7 subtract_add_fusion
  (28 shorter events, 1.9 us)
Async XLA Ops:
  0.0 2.2 %copy-start = (bf16[768,16]{0,1:T(8,128)(2,1)S(1)}, bf16[768,16]{0,1:T(8,128)(2,1)}, u32[]{:S(2)}) copy-start(bf16[768,16]{0,1:T(8,128)(2,1)} %param.8) | copy-start | bytes 73732
  27.3 0.8 copy-start.1
  27.5 0.7 copy-start.2
  27.5 0.7 copy-start.3
where the time goes:
time: 96.6 us; the launch traced here: 96 us
  blocking collectives  67.1 us (69%)
  matrix products  18.2 us (19%)
  other arithmetic  6.64 us (7%)
  local copies, waits for them, and re-layouts  3.74 us (4%)
    all_to_all x4, blocking collectives, per_device(): columns = lax.all_to_all(dev_total, 'time', 0, 0, tiled=True)  34.9 us
    all_to_all x4, blocking collectives, per_device(): lax.all_to_all(col_prefix, 'time', 0, 0, tiled=True).reshape(lat_shape)  32.2 us
    dot_general x4, matrix products, per_device(): jnp.einsum('kbnd,dc->kbnc', hidden, w_out, preferred_element_type=jnp.flo...  18.2 us
    another operation x4, other arithmetic, per_device(): local_cum = jnp.cumsum(drifts, axis=0)  2.8 us

commit v1 on v0

v1 whole, which is shorter than its diff:
```python
import functools

import jax
import jax.numpy as jnp
from jax import lax
from jax.experimental import pallas as pl
from jax.experimental.pallas import tpu as pltpu
from jax.sharding import PartitionSpec as P

SWEEPS = 4
F32, BF16 = jnp.float32, jnp.bfloat16
MESH = pl.DeviceIdType.MESH
LIN = 2 * 0.7978845608028654
CUB = 8 * 0.7978845608028654 * 0.044715


def kernel(n, x_ref, w_in_ref, w_out_ref, scale_ref, shift_ref, step_ref, out_ref,
           mods, first, first_send, lat, final, pre, mod_send, mod_recv, f_send, f_recv, o_send, o_recv):
    me = lax.axis_index("time")
    steps = scale_ref.shape[0]
    total = n * steps
    samples, chans, tokens = x_ref.shape
    hidden = w_in_ref.shape[1]
    width = samples * tokens // n
    per = tokens // width
    chips = n // per

    barrier = pltpu.get_barrier_semaphore()
    for d in range(1, n):
        pl.semaphore_signal(barrier, inc=1, device_id={"time": lax.rem(me + d, n)}, device_id_type=MESH)

    def place(dev):
        return dev // per, pl.ds(pl.multiple_of(lax.rem(dev, per) * width, width), width)

    for k in range(steps):
        mods[me, k:k + 1, :] = 0.5 * (1.0 + scale_ref[k:k + 1, :].astype(F32))
        mods[me, steps + k:steps + k + 1, :] = 0.5 * shift_ref[k:k + 1, :].astype(F32)
        mods[me, 2 * steps:2 * steps + 1, k * width:(k + 1) * width] = jnp.full((1, width), step_ref[k], F32)

    w_in = w_in_ref[...]
    w_out = w_out_ref[...]

    def up(slot, xt):
        pre[slot] = lax.dot_general(xt.astype(BF16), w_in, (((0,), (0,)), ((), ())), preferred_element_type=F32)

    def act(p, gain, shift):
        v = p * gain + shift
        return v + v * jnp.tanh(v * (v * v * CUB + LIN))

    def down(h):
        return lax.dot_general(w_out, h.astype(BF16), (((1,), (1,)), ((), ())), preferred_element_type=F32)

    pl.semaphore_wait(barrier, n - 1)
    mod_copies = []
    for d in range(1, n):
        dst = lax.rem(me + d, n)
        src = lax.rem(me + n - d, n)
        copy = pltpu.make_async_remote_copy(mods.at[me], mods.at[me], mod_send.at[d], mod_recv.at[d], device_id={"time": dst}, device_id_type=MESH)
        copy.start()
        mod_copies.append((copy, pltpu.make_async_remote_copy(mods.at[me], mods.at[src], mod_send.at[d], mod_recv.at[d], device_id={"time": dst}, device_id_type=MESH)))

    ring = sorted(range(chips), key=lambda d: -min(d, chips - d))
    f_copies = []
    my_chip = me // per
    up(0, x_ref[lax.rem(my_chip + ring[0], chips)])
    for i, d in enumerate(ring):
        chip = lax.rem(my_chip + d, chips)
        if i + 1 < chips:
            up((i + 1) % 2, x_ref[lax.rem(my_chip + ring[i + 1], chips)])
        p = pre[i % 2]
        for k in range(steps):
            f = down(act(p, mods[me, k:k + 1, :], mods[me, steps + k:steps + k + 1, :])) * step_ref[k]
            for c in range(per):
                first_send[chip * per + c, k] = f[:, c * width:(c + 1) * width]
        for c in range(per):
            if d == 0 and c == 0:
                first[me] = first_send[me]
                continue
            dst = chip * per + c if d else chip * per + lax.rem(lax.rem(me, per) + c, per)
            idx = d * per + c
            copy = pltpu.make_async_remote_copy(first_send.at[dst], first.at[me], f_send.at[idx], f_recv.at[me], device_id={"time": dst}, device_id_type=MESH)
            copy.start()
            f_copies.append(copy)

    for copy, arrival in mod_copies:
        copy.wait_send()
        arrival.wait_recv()
    for copy in f_copies:
        copy.wait_send()
    for d in range(1, n):
        src = lax.rem(me + d, n)
        pltpu.make_async_remote_copy(first_send.at[src], first.at[src], f_send.at[d], f_recv.at[src], device_id={"time": src}, device_id_type=MESH).wait_recv()

    mine_b, mine_l = place(me)
    x_mine = x_ref[mine_b, :, mine_l]

    def row(j, r):
        return mods[j // steps, r:r + 1, :]

    def drift_steps(j):
        k = j % steps
        return mods[j // steps, 2 * steps:2 * steps + 1, k * width:(k + 1) * width]

    run = x_mine + first[0, 0]
    for s in range(SWEEPS - 1):
        lat[s, 1] = run
    for j in range(1, total - 1):
        run = run + first[j // steps, j % steps]
        lat[0, j + 1] = run

    def pairs(s, todo):
        def load(j):
            return jnp.concatenate([lat[s, j], lat[s, j + 1]], axis=1)
        up(0, load(todo[0]))
        for i, j in enumerate(todo):
            if i + 1 < len(todo):
                up((i + 1) % 2, load(todo[i + 1]))
            p = pre[i % 2]
            h = []
            for c in range(2):
                k = (j + c) % steps
                h.append(act(p[c * width:(c + 1) * width], row(j + c, k), row(j + c, steps + k)))
            f = down(jnp.concatenate(h, axis=0))
            for c in range(2):
                prev = lat[s + 1, j + c] if s + 1 < SWEEPS - 1 else final[(j + c) // steps, (j + c) % steps]
                nxt = prev + f[:, c * width:(c + 1) * width] * drift_steps(j + c)
                if s + 1 < SWEEPS - 1:
                    lat[s + 1, j + c + 1] = nxt
                else:
                    final[(j + c + 1) // steps, (j + c + 1) % steps] = nxt

    everything = list(range(1, total - 1, 2))
    for s in range(SWEEPS - 2):
        pairs(s, everything)

    final[0, 0] = x_mine
    for j in range(1, SWEEPS):
        final[j // steps, j % steps] = lat[SWEEPS - 2, j]

    o_copies = []

    def send(q):
        copy = pltpu.make_async_remote_copy(final.at[q], out_ref.at[:, mine_b, :, mine_l], o_send.at[q], o_recv.at[me], device_id={"time": q}, device_id_type=MESH)

        @pl.when(me != q)
        def _():
            copy.start()

        @pl.when(me == q)
        def _():
            for k in range(steps):
                out_ref[k, mine_b, :, mine_l] = final[q, k]

    rest = everything[(SWEEPS - 1) // 2:]
    sent = 0
    for part in (rest[:4], rest[4:8], rest[8:]):
        pairs(SWEEPS - 2, part)
        while sent < n and (sent + 1) * steps - 1 <= part[-1] + 2:
            send(sent)
            sent += 1
    for q in range(n):
        copy = pltpu.make_async_remote_copy(final.at[q], out_ref.at[:, q // per, :, (q % per) * width:(q % per + 1) * width], o_send.at[q], o_recv.at[q], device_id={"time": q}, device_id_type=MESH)

        @pl.when(me != q)
        def _():
            copy.wait_send()
            copy.wait_recv()


def solution(mesh):
    n = mesh.shape["time"]

    def per_device(x_init, w_in, w_out, mod_scale, mod_shift, step_size):
        samples, tokens, chans = x_init.shape
        hidden = w_in.shape[1]
        steps = step_size.shape[0]
        total = n * steps
        width = samples * tokens // n
        rows = -(-(2 * steps + 1) // 8) * 8
        vmem = pl.BlockSpec(memory_space=pltpu.VMEM)
        out = pl.pallas_call(
            functools.partial(kernel, n),
            out_shape=jax.ShapeDtypeStruct((steps, samples, chans, tokens), F32),
            in_specs=[vmem] * 5 + [pl.BlockSpec(memory_space=pltpu.SMEM)],
            out_specs=vmem,
            scratch_shapes=[
                pltpu.VMEM((n, rows, hidden), F32),
                pltpu.VMEM((n, steps, chans, width), F32),
                pltpu.VMEM((n, steps, chans, width), F32),
                pltpu.VMEM((SWEEPS - 1, total, chans, width), F32),
                pltpu.VMEM((n, steps, chans, width), F32),
                pltpu.VMEM((2, 2 * width, hidden), F32),
                pltpu.SemaphoreType.DMA((n,)),
                pltpu.SemaphoreType.DMA((n,)),
                pltpu.SemaphoreType.DMA((n,)),
                pltpu.SemaphoreType.DMA((n,)),
                pltpu.SemaphoreType.DMA((n,)),
                pltpu.SemaphoreType.DMA((n,)),
            ],
            compiler_params=pltpu.CompilerParams(collective_id=0, has_side_effects=True),
        )(jnp.transpose(x_init, (0, 2, 1)), w_in, w_out.T, mod_scale, mod_shift, step_size)
        return jnp.transpose(out, (0, 1, 3, 2))

    return jax.shard_map(per_device, mesh=mesh, in_specs=(P('data'), P(), P(), P('time'), P('time'), P('time')), out_specs=P('time', 'data'), check_vma=False)
```

time: 96.6 us -> 26.2 us (0.27)
  the two profiles are of different devices: /device:TPU:112 before, /device:TPU:113 now
where the time goes in v1:
time: 26.2 us; the launch traced here: 26 us
  Pallas kernels  24.4 us (93%)
  local copies, waits for them, and re-layouts  1.62 us (6%)
    pallas_call x1, Pallas kernels, per_device(): pl.pallas_call(functools.partial(kernel, n), out_shape=jax.ShapeDtypeStru...  24.4 us
    unnamed x1, local copies, waits for them, and re-layouts  1.62 us

profile of v1, /device:TPU:113, one launch (start us, length us, event | category | flops | bytes accessed | tf_op | source)
XLA Modules:
  0.0 26.0 jit_solution(15332614006677992368)
XLA Ops:
  0.0 24.4 %shard_map.64 = f32[3,4,16,256]{3,2,1,0:T(8,128)} custom-call(f32[4,16,256]{2,1,0:T(8,128)} %bitcast.4, bf16[16,768]{1,0:T(8,128)(2,1)} %w_in_ref.1, bf16[16,768]{1,0:T(8,128)(2,1)} %bitcast.5, bf16[3,768]{1,0:T(4,128)(2,1)} %scale_ref.1, bf16[3,768]{1,0:T(4,128)(2,1)} %shift_ref.1, f32[3]{0:T(128)} %step_ref.1), custom_call_target="tpu_custom_call" | custom-call | tf_op jit(solution)/shard_map/pallas_call | solution.py:181
  24.4 1.6 %copy.8 = f32[3,4,256,16]{2,3,1,0:T(8,128)} copy(f32[3,4,256,16]{2,3,1,0:T(8,128)} %bitcast.3) | data formatting | bytes 393216

commit v2 on v0

v2 whole, which is shorter than its diff:
```python
import functools

import jax
import jax.numpy as jnp
from jax import lax
from jax.experimental import pallas as pl
from jax.experimental.pallas import tpu as pltpu
from jax.sharding import PartitionSpec as P

SWEEPS = 4
F32, BF16 = jnp.float32, jnp.bfloat16
MESH = pl.DeviceIdType.MESH
LIN = 2 * 0.7978845608028654
CUB = 8 * 0.7978845608028654 * 0.044715


def kernel(n, x_hbm, w_in_hbm, w_out_hbm, scale_hbm, shift_hbm, step_hbm, out_ref,
           x_ref, w_in_ref, w_out_ref, rows, sizes, gains, hs, first, first_send, lat, final, pre,
           load_sem, row_send, row_recv, size_send, size_recv, f_send, f_recv, o_send, o_recv):
    me = lax.axis_index("time")
    steps = scale_hbm.shape[0]
    total = n * steps
    samples, chans, tokens = x_hbm.shape
    width = samples * tokens // n
    per = tokens // width
    chips = n // per

    barrier = pltpu.get_barrier_semaphore()
    for d in range(1, n):
        pl.semaphore_signal(barrier, inc=1, device_id={"time": lax.rem(me + d, n)}, device_id_type=MESH)

    mine_b, mine_l = me // per, pl.ds(pl.multiple_of(lax.rem(me, per) * width, width), width)
    loads = [pltpu.make_async_copy(src, dst, load_sem.at[i]) for i, (src, dst) in enumerate([
        (scale_hbm, rows.at[me, 0]), (shift_hbm, rows.at[me, 1]), (x_hbm, x_ref), (w_in_hbm, w_in_ref), (w_out_hbm, w_out_ref), (step_hbm, sizes.at[me])])]
    for copy in loads:
        copy.start()

    def up(xt):
        return lax.dot_general(xt.astype(BF16), w_in_ref[...], (((0,), (0,)), ((), ())), preferred_element_type=F32)

    def act(p, gain, shift):
        v = p * gain + shift
        return v + v * jnp.tanh(v * (v * v * CUB + LIN))

    def down(h):
        return lax.dot_general(w_out_ref[...], jnp.concatenate(h, axis=0).astype(BF16), (((1,), (1,)), ((), ())), preferred_element_type=F32)

    def unpack(q):
        gains[q, 0] = 0.5 * (1.0 + rows[q, 0].astype(F32))
        gains[q, 1] = 0.5 * rows[q, 1].astype(F32)
        for k in range(steps):
            hs[q, k:k + 1] = jnp.broadcast_to(sizes[q, :, k:k + 1], (1, width))

    for copy in loads:
        copy.wait()
    unpack(me)

    ring = [0] + [d for d in sorted(range(chips), key=lambda d: min(d, chips - d)) if d]
    my_chip, my_core = me // per, lax.rem(me, per)
    sent = []

    def push(src, dst, send_sem, recv_sem, q):
        copy = pltpu.make_async_remote_copy(src, dst, send_sem, recv_sem, device_id={"time": q}, device_id_type=MESH)
        copy.start()
        sent.append(copy)

    pre[0] = up(x_ref[lax.rem(my_chip + ring[0], chips)])
    for i, d in enumerate(ring):
        chip = lax.rem(my_chip + d, chips)
        if i + 1 < chips:
            pre[(i + 1) % 2] = up(x_ref[lax.rem(my_chip + ring[i + 1], chips)])
        p = pre[i % 2]
        for k in range(steps):
            f = down([act(p, gains[me, 0, k:k + 1], gains[me, 1, k:k + 1])])
            for c in range(per):
                first_send[chip * per + c, k] = f[:, c * width:(c + 1) * width] * hs[me, k:k + 1]
        if i == 1:
            pl.semaphore_wait(barrier, n - 1)
            for e in sorted(range(1, n), key=lambda e: (min(e // per, chips - e // per), e)):
                q = lax.rem(my_chip + e // per, chips) * per + lax.rem(my_core + e % per, per)
                push(rows.at[me], rows.at[me], row_send.at[q], row_recv.at[me], q)
                push(sizes.at[me], sizes.at[me], size_send.at[q], size_recv.at[me], q)
        for c in range(per):
            if not (d or c):
                first[me] = first_send[me]
        for e in list(ring[:i + 1] if i == 1 else ring[i:i + 1] if i > 1 else []):
            for c in range(per):
                if e or c:
                    q = lax.rem(my_chip + e, chips) * per + lax.rem(my_core + c, per)
                    push(first_send.at[q], first.at[me], f_send.at[q], f_recv.at[me], q)

    x_mine = x_ref[mine_b, :, mine_l]
    lat[0, 0] = x_mine
    final[0, 0] = x_mine
    here = []

    def need(j):
        while len(here) * steps <= j:
            group = [len(here) + c for c in range(per)]
            for q in group:
                @pl.when(me != q)
                def _():
                    for ref, send_sem, recv_sem in ((rows, row_send, row_recv), (sizes, size_send, size_recv), (first, f_send, f_recv)):
                        pltpu.make_async_remote_copy(ref.at[q], ref.at[q], send_sem.at[q], recv_sem.at[q], device_id={"time": q}, device_id_type=MESH).wait_recv()
            for q in group:
                here.append(q)
                unpack(q)
                for k in range(steps):
                    j0 = q * steps + k
                    if j0 + 1 < total:
                        lat[0, j0 + 1] = lat[0, j0] + first[q, k]
                    if not j0:
                        for s in range(1, SWEEPS - 1):
                            lat[s, 1] = lat[0, 1]
                        final[0, 1] = lat[0, 1]

    def send(lo, hi):
        q, a, b = lo // steps, lo % steps, hi - lo // steps * steps
        copy = pltpu.make_async_remote_copy(final.at[q, a:b], out_ref.at[a:b, mine_b, :, mine_l], o_send.at[lo], o_recv.at[me, a], device_id={"time": q}, device_id_type=MESH)

        @pl.when(me != q)
        def _():
            copy.start()

        @pl.when(me == q)
        def _():
            for k in range(a, b):
                out_ref[k, mine_b, :, mine_l] = final[q, k]

    def load(item):
        s, j = item
        return jnp.concatenate([lat[s, j], lat[s, j + 1]], axis=1)

    def finish(slot, item):
        s, j = item
        last = s + 2 == SWEEPS
        p = pre[slot]
        pair = [(c, (j + c) // steps, (j + c) % steps) for c in range(2)]
        f = down([act(p[c * width:(c + 1) * width], gains[q, 0, k:k + 1], gains[q, 1, k:k + 1]) for c, q, k in pair])
        for c, q, k in pair:
            nxt = (final[q, k] if last else lat[s + 1, j + c]) + f[:, c * width:(c + 1) * width] * hs[q, k:k + 1]
            if last:
                final[(j + c + 1) // steps, (j + c + 1) % steps] = nxt
            else:
                lat[s + 1, j + c + 1] = nxt
            if s + 1 == j + c:
                final[(j + c + 1) // steps, (j + c + 1) % steps] = nxt

    starts = list(range(1, total - 1, 2))
    items = []
    for t in range(len(starts) + SWEEPS - 2):
        for s in range(SWEEPS - 1):
            if 0 <= t - s < len(starts) and starts[t - s] + 1 > s:
                items.append((s, starts[t - s]))
    cuts = (total - 15, total - 7, total - 5)
    need(items[0][1] + 1)
    pre[0] = up(load(items[0]))
    gone = 0
    sizes_sent = []
    for i, item in enumerate(items):
        if i + 1 < len(items):
            need(items[i + 1][1] + 1)
            pre[(i + 1) % 2] = up(load(items[i + 1]))
        finish(i % 2, item)
        s, j = item
        if s + 2 == SWEEPS and j in cuts or i + 1 == len(items):
            ready = j + 3
            while gone < ready:
                upto = min(ready, (gone // steps + 1) * steps)
                if upto % steps and j not in cuts[-1:] and i + 1 < len(items):
                    break
                send(gone, upto)
                sizes_sent.append((gone, upto))
                gone = upto

    for copy in sent:
        copy.wait_send()
    for lo, hi in sizes_sent:
        q, a, b = lo // steps, lo % steps, hi - lo // steps * steps

        @pl.when(me != q)
        def _():
            pltpu.make_async_remote_copy(final.at[q, a:b], out_ref.at[a:b, mine_b, :, mine_l], o_send.at[lo], o_recv.at[me, a], device_id={"time": q}, device_id_type=MESH).wait_send()

        @pl.when(me == q)
        def _():
            for d in range(1, n):
                src = lax.rem(me + d, n)
                src_l = pl.ds(pl.multiple_of(lax.rem(src, per) * width, width), width)
                pltpu.make_async_remote_copy(final.at[q, a:b], out_ref.at[a:b, src // per, :, src_l], o_send.at[lo], o_recv.at[src, a], device_id={"time": src}, device_id_type=MESH).wait_recv()


def solution(mesh):
    n = mesh.shape["time"]

    def per_device(x_init, w_in, w_out, mod_scale, mod_shift, step_size):
        samples, tokens, chans = x_init.shape
        hidden = w_in.shape[1]
        steps = step_size.shape[0]
        total = n * steps
        width = samples * tokens // n
        anywhere = pl.BlockSpec(memory_space=pl.ANY)
        dma = pltpu.SemaphoreType.DMA
        out = pl.pallas_call(
            functools.partial(kernel, n),
            out_shape=pltpu.VMEM((steps, samples, chans, tokens), F32),
            in_specs=[anywhere] * 6,
            out_specs=pl.BlockSpec(memory_space=pltpu.VMEM),
            scratch_shapes=[
                pltpu.VMEM((samples, chans, tokens), F32),
                pltpu.VMEM((chans, hidden), BF16),
                pltpu.VMEM((chans, hidden), BF16),
                pltpu.VMEM((n, 2, steps, hidden), BF16),
                pltpu.VMEM((n, 1, steps), F32),
                pltpu.VMEM((n, 2, steps, hidden), F32),
                pltpu.VMEM((n, steps, width), F32),
                pltpu.VMEM((n, steps, chans, width), F32),
                pltpu.VMEM((n, steps, chans, width), F32),
                pltpu.VMEM((SWEEPS - 1, total, chans, width), F32),
                pltpu.VMEM((n, steps, chans, width), F32),
                pltpu.VMEM((2, 2 * width, hidden), F32),
                dma((6,)), dma((n,)), dma((n,)), dma((n,)), dma((n,)), dma((n,)), dma((n,)), dma((total,)), dma((n, steps)),
            ],
            compiler_params=pltpu.CompilerParams(collective_id=0, has_side_effects=True),
        )(jnp.transpose(x_init, (0, 2, 1)), w_in, w_out.T, mod_scale, mod_shift, step_size[None])
        return jnp.transpose(out, (0, 1, 3, 2))

    return jax.shard_map(per_device, mesh=mesh, in_specs=(P('data'), P(), P(), P('time'), P('time'), P('time')), out_specs=P('time', 'data'), check_vma=False)
```

time: 96.6 us -> 21.4 us (0.22)
  the two profiles are of different devices: /device:TPU:112 before, /device:TPU:119 now
where the time goes in v2:
time: 21.4 us; the launch traced here: 21.3 us
  Pallas kernels  20.6 us (96%)
  local copies, waits for them, and re-layouts  0.68 us (3%)
    pallas_call x1, Pallas kernels, per_device(): pl.pallas_call(functools.partial(kernel, n), out_shape=pltpu.VMEM((steps,...  20.6 us
    unnamed x1, local copies, waits for them, and re-layouts  0.68 us

profile of v2, /device:TPU:119, one launch (start us, length us, event | category | flops | bytes accessed | tf_op | source)
XLA Modules:
  0.0 21.3 jit_solution(1745252630459687396)
XLA Ops:
  0.0 20.6 %shard_map.64 = f32[3,4,16,256]{3,2,1,0:T(8,128)S(1)} custom-call(f32[4,16,256]{2,1,0:T(8,128)} %bitcast.5, bf16[16,768]{1,0:T(8,128)(2,1)} %w_in_hbm.1, bf16[16,768]{1,0:T(8,128)(2,1)} %bitcast.6, bf16[3,768]{1,0:T(4,128)(2,1)} %scale_hbm.1, bf16[3,768]{1,0:T(4,128)(2,1)} %shift_hbm.1, f32[1,3]{1,0:T(1,128)} %bitcast.7), custom_call_target="tpu_custom_call" | custom-call | tf_op jit(solution)/shard_map/pallas_call | solution.py:204
  20.6 0.7 %copy.8 = f32[3,4,256,16]{2,3,1,0:T(8,128)} copy(f32[3,4,256,16]{2,3,1,0:T(8,128)S(1)} %bitcast.4) | data formatting | bytes 393216

commit v3 on v2

--- a/solution.py
+++ b/solution.py
@@ -143,15 +143,13 @@
                 final[(j + c + 1) // steps, (j + c + 1) % steps] = nxt
             else:
                 lat[s + 1, j + c + 1] = nxt
-            if s + 1 == j + c:
-                final[(j + c + 1) // steps, (j + c + 1) % steps] = nxt
-
-    starts = list(range(1, total - 1, 2))
-    items = []
-    for t in range(len(starts) + SWEEPS - 2):
-        for s in range(SWEEPS - 1):
-            if 0 <= t - s < len(starts) and starts[t - s] + 1 > s:
-                items.append((s, starts[t - s]))
+            if j + c == s + 1:
+                if not last:
+                    final[(j + c + 1) // steps, (j + c + 1) % steps] = nxt
+                if s + 2 < SWEEPS - 1:
+                    lat[s + 2, j + c + 1] = nxt
+
+    items = [(s - 1, s + 2 * (t - s)) for t in range(total) for s in range(1, SWEEPS) if 0 <= t - s < (total - SWEEPS) // 2]
     cuts = (total - 15, total - 7, total - 5)
     need(items[0][1] + 1)
     pre[0] = up(load(items[0]))

time: 21.4 us -> 20.8 us (0.972)
  Pallas kernels: 20.6 us -> 20 us
    pallas_call x1, Pallas kernels: 20.6 us -> 20 us  [per_device(): pl.pallas_call(functools.partial(kernel, n), out_shape=pltpu.VMEM((steps,...]
where the time goes in v3:
time: 20.8 us; the launch traced here: 20.7 us
  Pallas kernels  20 us (96%)
  local copies, waits for them, and re-layouts  0.68 us (3%)
    pallas_call x1, Pallas kernels, per_device(): pl.pallas_call(functools.partial(kernel, n), out_shape=pltpu.VMEM((steps,...  20 us
    unnamed x1, local copies, waits for them, and re-layouts  0.68 us

profile of v3, /device:TPU:119, one launch (start us, length us, event | category | flops | bytes accessed | tf_op | source)
XLA Modules:
  0.0 20.7 jit_solution(12732222081623285678)
XLA Ops:
  0.0 20.0 %shard_map.64 = f32[3,4,16,256]{3,2,1,0:T(8,128)S(1)} custom-call(f32[4,16,256]{2,1,0:T(8,128)} %bitcast.5, bf16[16,768]{1,0:T(8,128)(2,1)} %w_in_hbm.1, bf16[16,768]{1,0:T(8,128)(2,1)} %bitcast.6, bf16[3,768]{1,0:T(4,128)(2,1)} %scale_hbm.1, bf16[3,768]{1,0:T(4,128)(2,1)} %shift_hbm.1, f32[1,3]{1,0:T(1,128)} %bitcast.7), custom_call_target="tpu_custom_call" | custom-call | tf_op jit(solution)/shard_map/pallas_call | solution.py:202
  20.0 0.7 %copy.8 = f32[3,4,256,16]{2,3,1,0:T(8,128)} copy(f32[3,4,256,16]{2,3,1,0:T(8,128)S(1)} %bitcast.4) | data formatting | bytes 393216

commit v4 on v3

--- a/solution.py
+++ b/solution.py
@@ -96,7 +96,7 @@
 
     def need(j):
         while len(here) * steps <= j:
-            group = [len(here) + c for c in range(per)]
+            group = [len(here) + c for c in range(per if len(here) < 2 * per else n - 2 * per)]
             for q in group:
                 @pl.when(me != q)
                 def _():
@@ -121,11 +121,6 @@
         @pl.when(me != q)
         def _():
             copy.start()
-
-        @pl.when(me == q)
-        def _():
-            for k in range(a, b):
-                out_ref[k, mine_b, :, mine_l] = final[q, k]
 
     def load(item):
         s, j = item
@@ -150,7 +145,7 @@
                     lat[s + 2, j + c + 1] = nxt
 
     items = [(s - 1, s + 2 * (t - s)) for t in range(total) for s in range(1, SWEEPS) if 0 <= t - s < (total - SWEEPS) // 2]
-    cuts = (total - 15, total - 7, total - 5)
+    cuts = (total - 15, total - 7)
     need(items[0][1] + 1)
     pre[0] = up(load(items[0]))
     gone = 0
@@ -171,6 +166,8 @@
                 sizes_sent.append((gone, upto))
                 gone = upto
 
+    for k in range(steps):
+        out_ref[k, mine_b, :, mine_l] = final[me, k]
     for copy in sent:
         copy.wait_send()
     for lo, hi in sizes_sent:

time: 20.8 us -> 20.4 us (0.981)
  Pallas kernels: 20 us -> 19.6 us
    pallas_call x1, Pallas kernels: 20 us -> 19.6 us  [per_device(): pl.pallas_call(functools.partial(kernel, n), out_shape=pltpu.VMEM((steps,...]
where the time goes in v4:
time: 20.4 us; the launch traced here: 20.3 us
  Pallas kernels  19.6 us (96%)
  local copies, waits for them, and re-layouts  0.68 us (3%)
    pallas_call x1, Pallas kernels, per_device(): pl.pallas_call(functools.partial(kernel, n), out_shape=pltpu.VMEM((steps,...  19.6 us
    unnamed x1, local copies, waits for them, and re-layouts  0.68 us

profile of v4, /device:TPU:119, one launch (start us, length us, event | category | flops | bytes accessed | tf_op | source)
XLA Modules:
  0.0 20.3 jit_solution(15667714724856644365)
XLA Ops:
  0.0 19.6 %shard_map.64 = f32[3,4,16,256]{3,2,1,0:T(8,128)S(1)} custom-call(f32[4,16,256]{2,1,0:T(8,128)} %bitcast.5, bf16[16,768]{1,0:T(8,128)(2,1)} %w_in_hbm.1, bf16[16,768]{1,0:T(8,128)(2,1)} %bitcast.6, bf16[3,768]{1,0:T(4,128)(2,1)} %scale_hbm.1, bf16[3,768]{1,0:T(4,128)(2,1)} %shift_hbm.1, f32[1,3]{1,0:T(1,128)} %bitcast.7), custom_call_target="tpu_custom_call" | custom-call | tf_op jit(solution)/shard_map/pallas_call | solution.py:199
  19.6 0.7 %copy.8 = f32[3,4,256,16]{2,3,1,0:T(8,128)} copy(f32[3,4,256,16]{2,3,1,0:T(8,128)S(1)} %bitcast.4) | data formatting | bytes 393216

commit v5 on v4

--- a/solution.py
+++ b/solution.py
@@ -51,9 +51,8 @@
         for k in range(steps):
             hs[q, k:k + 1] = jnp.broadcast_to(sizes[q, :, k:k + 1], (1, width))
 
-    for copy in loads:
+    for copy in loads[2:4]:
         copy.wait()
-    unpack(me)
 
     ring = [0] + [d for d in sorted(range(chips), key=lambda d: min(d, chips - d)) if d]
     my_chip, my_core = me // per, lax.rem(me, per)
@@ -65,6 +64,9 @@
         sent.append(copy)
 
     pre[0] = up(x_ref[lax.rem(my_chip + ring[0], chips)])
+    for copy in loads[:2] + loads[4:]:
+        copy.wait()
+    unpack(me)
     for i, d in enumerate(ring):
         chip = lax.rem(my_chip + d, chips)
         if i + 1 < chips:

time: 20.4 us -> 20.4 us (level)
  no operation moved by 1% of the time
where the time goes in v5:
time: 20.4 us; the launch traced here: 20.3 us
  Pallas kernels  19.6 us (96%)
  local copies, waits for them, and re-layouts  0.68 us (3%)
    pallas_call x1, Pallas kernels, per_device(): pl.pallas_call(functools.partial(kernel, n), out_shape=pltpu.VMEM((steps,...  19.6 us
    unnamed x1, local copies, waits for them, and re-layouts  0.68 us

profile of v5, /device:TPU:119, one launch (start us, length us, event | category | flops | bytes accessed | tf_op | source)
XLA Modules:
  0.0 20.3 jit_solution(3806307497472493773)
XLA Ops:
  0.0 19.6 %shard_map.64 = f32[3,4,16,256]{3,2,1,0:T(8,128)S(1)} custom-call(f32[4,16,256]{2,1,0:T(8,128)} %bitcast.5, bf16[16,768]{1,0:T(8,128)(2,1)} %w_in_hbm.1, bf16[16,768]{1,0:T(8,128)(2,1)} %bitcast.6, bf16[3,768]{1,0:T(4,128)(2,1)} %scale_hbm.1, bf16[3,768]{1,0:T(4,128)(2,1)} %shift_hbm.1, f32[1,3]{1,0:T(1,128)} %bitcast.7), custom_call_target="tpu_custom_call" | custom-call | tf_op jit(solution)/shard_map/pallas_call | solution.py:201
  19.6 0.7 %copy.8 = f32[3,4,256,16]{2,3,1,0:T(8,128)} copy(f32[3,4,256,16]{2,3,1,0:T(8,128)S(1)} %bitcast.4) | data formatting | bytes 393216
